TPU v7x, 32 devices: a whole 2x2x4 slice. The times are simulated.
32 devices in a mesh: seq: 8 (over z, x), head: 4 (over y, core).
Axes of the slice: x: 2, y: 2, z: 4, core: 2. Of those that a mesh axis runs over, the one named last changes fastest.
Arguments:
- inputs: float32 [4096, 2048], P('seq'), may hold values from -6 to 6
- decay_exponent: int32 [8], P('head'), may hold values from 5 to 18, as said below
- first_gain: bfloat16 [2048], P('seq'), may hold values from 0.099609375 to 1.8984375
- first_bias: bfloat16 [2048], P('seq'), may hold values from -3 to 3
- query_weight: bfloat16 [2048, 2048], P('seq', 'head'), may hold values from -0.125 to 0.125
- key_weight: bfloat16 [2048, 2048], P('seq', 'head'), may hold values from -0.125 to 0.125
- value_weight: bfloat16 [2048, 4096], P('seq', 'head'), may hold values from -0.125 to 0.125
- gate_weight: bfloat16 [2048, 4096], P('seq', 'head'), may hold values from -0.125 to 0.125
- out_weight: bfloat16 [4096, 2048], P('head', 'seq'), may hold values from -0.09375 to 0.09375
- second_gain: bfloat16 [2048], P('seq'), may hold values from 0.099609375 to 1.8984375
- second_bias: bfloat16 [2048], P('seq'), may hold values from -3 to 3
- up_weight: bfloat16 [2048, 4096], P('seq', 'head'), may hold values from -0.125 to 0.125
- down_weight: bfloat16 [4096, 2048], P('head', 'seq'), may hold values from -0.09375 to 0.09375
- cotangent: float32 [4096, 2048], P('seq', 'head'), may hold values from -6 to 6
Outputs:
- layer_out: float32 [4096, 2048], P('seq', 'head')
- grad_inputs: float32 [4096, 2048], P('seq', 'head')
- grad_first_gain: float32 [2048], P('seq')
- grad_first_bias: float32 [2048], P('seq')
- grad_query_weight: float32 [2048, 2048], P('seq', 'head')
- grad_key_weight: float32 [2048, 2048], P('seq', 'head')
- grad_value_weight: float32 [2048, 4096], P('seq', 'head')
- grad_gate_weight: float32 [2048, 4096], P('seq', 'head')
- grad_out_weight: float32 [4096, 2048], P('head', 'seq')
- grad_second_gain: float32 [2048], P('seq')
- grad_second_bias: float32 [2048], P('seq')
- grad_up_weight: float32 [2048, 4096], P('seq', 'head')
- grad_down_weight: float32 [4096, 2048], P('head', 'seq')
Inputs may be any that keep to these rules, and one draw needn't show every extreme that they name: `decay_exponent`: holds each of 5, 6, 8, 11, 15, 16, 17 and 18 once, in an order drawn from the seed.
All inputs are finite; a program needn't handle non-finite values.
Results may differ from a plain program's by a relative error of at most 0.02.
Values may be sent and summed in bfloat16 or wider, within the bound.
A program may use at most 256 MiB of HBM per device.

v0:
```python
import functools
import math
import types

import jax
import jax.numpy as jnp
import numpy as np
from jax import lax
from jax.experimental import pallas as pl
from jax.experimental.pallas import tpu as pltpu
from jax.sharding import Mesh, PartitionSpec as P

EPSILON = 1e-05
BF = jnp.bfloat16
F32 = jnp.float32
MESH = pl.DeviceIdType.MESH
VMEM_LIMIT = 67043328

def pick(array, index, axis):
    return lax.dynamic_index_in_dim(array, index, axis, keepdims=False)


def dot(left, right, contract):
    return lax.dot_general(left, right, (contract, ((), ())), preferred_element_type=F32)


def mm(left, right):
    return dot(left, right, ((1,), (0,)))


def mm_t(left, right):
    return dot(left, right, ((1,), (1,)))


def t_mm(left, right):
    return dot(left, right, ((0,), (0,)))


class Plan:
    def __init__(self, seq_bits, head_bits):
        self.seq = [f"s{i}" for i in range(seq_bits)]
        self.head = [f"h{i}" for i in range(head_bits)]
        self.names = tuple(reversed(self.seq)) + ()
        self.seq_axes = tuple(reversed(self.seq))
        self.head_axes = tuple(reversed(self.head))
        self.pair = "s1" if seq_bits > 1 else "s0"
        self.low = [a for a in self.seq if a < self.pair]
        self.high = [a for a in self.seq if a > self.pair]


class Square:
    def __init__(self, pair):
        self.pair = pair
        self.p = lax.axis_index(pair)
        self.y = lax.axis_index("h1")
        self.c = lax.axis_index("h0")
        self.S = {pair: 1 - self.p}
        self.Y = {"h1": 1 - self.y}
        self.C = {"h0": 1 - self.c}
        self.X = {"h1": 1 - self.y, "h0": 1 - self.c}

    def greet(self, cross=True):
        barrier = pltpu.get_barrier_semaphore()
        peers = [self.S, self.Y, self.C] + ([self.X] if cross else [])
        for peer in peers:
            pl.semaphore_signal(barrier, inc=1, device_id=peer, device_id_type=MESH)
        pl.semaphore_wait(barrier, len(peers))


def remote(source, target, sends, receives, index, device):
    return pltpu.make_async_remote_copy(
        src_ref=source,
        dst_ref=target,
        send_sem=sends.at[index],
        recv_sem=receives.at[index],
        device_id=device,
        device_id_type=MESH,
    )


def spread(sq, block, full, sends, receives, base, local_sem):
    rows, width = block.shape
    half = rows // 2

    def place(p, y, c, start, count):
        return full.at[p, pl.ds(start, count), pl.ds(pl.multiple_of((y * 2 + c) * width, width), width)]

    p, y, c = sq.p, sq.y, sq.c
    top, low = (0, half), (half, half)

    def own(part):
        return block.at[pl.ds(part[0], part[1]), :]

    def send(index, source, target, device):
        copy = remote(source, target, sends, receives, base + index, device)
        copy.start()
        return copy

    def relay(index, p_, y_, part, device):
        return send(index, place(p_, y_, c, *part), place(p_, y_, c, *part), device)

    k0 = send(0, own(top), place(p, y, c, *top), sq.S)
    k2 = send(2, own(low), place(p, y, c, *low), sq.Y)
    k6 = send(6, block, place(p, y, c, 0, rows), sq.C)
    k1 = send(1, own(low), place(p, y, c, *low), sq.S)
    k3 = send(3, own(top), place(p, y, c, *top), sq.Y)
    keep = pltpu.make_async_copy(block, place(p, y, c, 0, rows), local_sem)
    keep.start()
    k2.wait_recv()
    k4 = relay(4, p, 1 - y, low, sq.S)
    k9 = relay(9, p, 1 - y, low, sq.C)
    k0.wait_recv()
    k5 = relay(5, 1 - p, y, top, sq.Y)
    k7 = relay(7, 1 - p, y, top, sq.C)
    k1.wait_recv()
    k8 = relay(8, 1 - p, y, low, sq.C)
    k3.wait_recv()
    k10 = relay(10, p, 1 - y, top, sq.C)
    k5.wait_recv()
    k11 = relay(11, 1 - p, 1 - y, top, sq.C)
    k4.wait_recv()
    k12 = relay(12, 1 - p, 1 - y, low, sq.C)
    for copy in (k6, k7, k8, k9, k10, k11, k12):
        copy.wait_recv()
    for copy in (k0, k1, k2, k3, k4, k5, k6, k7, k8, k9, k10, k11, k12):
        copy.wait_send()
    keep.wait()


SPREAD_COPIES = 13
REDUCE_COPIES = 10


def exchange(sq, first, second, stats, sends, receives, base):
    rows = first.shape[0]
    lane = lax.broadcasted_iota(jnp.int32, (rows, 128), 1)
    packed = jnp.where(lane == 0, first, second).T
    mine = sq.y * 2 + sq.c
    stats[mine] = packed[:8]
    copies = []
    for index, device in enumerate((sq.Y, sq.C, sq.X)):
        copy = remote(stats.at[mine], stats.at[mine], sends, receives, base + index, device)
        copy.start()
        copies.append(copy)
    for copy in copies:
        copy.wait_recv()
    for copy in copies:
        copy.wait_send()
    return [stats[q][0:1] for q in range(4)], [stats[q][1:2] for q in range(4)]


def upright(first, second):
    rows = first.shape[1]
    line = lax.broadcasted_iota(jnp.int32, (128, rows), 0)
    turned = jnp.where(line == 0, first, second).T
    return turned[:, 0:1], turned[:, 1:2]


class Bulk:
    def __init__(self, plan, at, shards, wholes, sends, receives, local_sem):
        self.shards, self.wholes, self.at = shards, wholes, at
        self.sends, self.receives, self.local_sem = sends, receives, local_sem
        self.axes = [plan.pair] + plan.high + plan.low
        self.high, self.low, self.lows = plan.high, plan.low, len(plan.low)
        self.bit = {axis: 1 << plan.seq.index(axis) for axis in self.axes}
        self.me = sum(at[axis] * self.bit[axis] for axis in self.axes)
        self.size = 1 << len(self.axes)
        self.copies, self.kept, self.passed = [], {}, set()

    def piece(self, unit, mask):
        rows = self.shards[unit].shape[0]
        return self.wholes[unit].at[pl.ds(pl.multiple_of((self.me ^ mask) * rows, rows), rows), :]

    def half(self, unit, which):
        width = self.wholes[unit].shape[1]
        return self.shards[unit].at[:, pl.ds(pl.multiple_of(which * width, width), width)]

    def link(self, unit, source, held, axis):
        return remote(
            source,
            self.piece(unit, held),
            self.sends,
            self.receives,
            unit * self.size + (held | self.bit[axis]),
            {axis: 1 - self.at[axis]},
        )

    def send(self, unit, source, held, axis):
        copy = self.link(unit, source, held, axis)
        copy.start()
        self.copies.append(copy)

    def begin(self, unit, axes):
        own = self.at[self.axes[0]]
        for axis in axes:
            self.send(unit, self.half(unit, 1 - own if axis == self.axes[0] else own), 0, axis)
        if self.axes[0] in axes:
            keep = pltpu.make_async_copy(self.half(unit, own), self.piece(unit, 0), self.local_sem.at[unit])
            keep.start()
            self.kept[unit] = keep

    def held_before(self, stage):
        held = [0]
        for axis in self.axes[:stage]:
            held = held + [m | self.bit[axis] for m in held]
        return held

    def forward(self, unit, mask, axes):
        for later in axes:
            self.send(unit, self.piece(unit, mask), mask, later)

    def arrive(self, unit, stage, masks, axes=None):
        axis = self.axes[stage]
        for held in self.held_before(stage):
            mask = held | self.bit[axis]
            if not masks(mask):
                continue
            pltpu.make_async_remote_copy(
                src_ref=self.piece(unit, mask),
                dst_ref=self.piece(unit, mask),
                send_sem=self.sends.at[unit * self.size + mask],
                recv_sem=self.receives.at[unit * self.size + mask],
                device_id={axis: 1 - self.at[axis]},
                device_id_type=MESH,
            ).wait_recv()
            self.forward(unit, mask, self.axes[stage + 1 :] if axes is None else axes)

    def paired(self, unit, axes=None):
        self.arrive(unit, 0, lambda mask: True, axes)

    def first(self, unit):
        for stage in range(1, len(self.axes) - self.lows):
            self.arrive(unit, stage, lambda mask: not mask & self.bit[self.axes[0]])

    def second(self, unit):
        for stage in range(1, len(self.axes) - self.lows):
            self.arrive(unit, stage, lambda mask: mask & self.bit[self.axes[0]])

    def finish(self, unit):
        for stage in range(len(self.axes) - self.lows, len(self.axes)):
            self.arrive(unit, stage, lambda mask: True)
        self.kept[unit].wait()

    def drain(self):
        for copy in self.copies:
            copy.wait_send()


def together(process, *hooks):
    for number, _ in enumerate(process):
        if number < len(hooks):
            hooks[number]()


def carried(plan, at, state, reach, low_buf, high_buf, rate, length, reverse, sends, receives, base):
    index = base
    low_index = jnp.float32(0)
    span = 1.0
    copies = []

    def decay(count):
        return jnp.exp(rate * (count * float(length)))

    for slot in range(2):
        reach[slot] = jnp.zeros(reach.shape[1:], F32)
    for number, axis in enumerate(plan.low):
        bit = at[axis].astype(F32)
        late = 1.0 - bit if reverse else bit
        for slot in range(2):
            low_buf[2 * number, slot] = state[slot].astype(BF)
        copy = remote(low_buf.at[2 * number], low_buf.at[2 * number + 1], sends, receives, index, {axis: 1 - at[axis]})
        copy.start()
        copies.append(copy)
        index += 1
        yield
        copy.wait_recv()
        between = span - 1.0 - low_index if reverse else low_index
        step_decay = decay(span)
        take, keep = late * step_decay + (1.0 - late), late + (1.0 - late) * step_decay
        for slot in range(2):
            got = low_buf[2 * number + 1, slot].astype(F32)
            reach[slot] += got * (late * decay(between))
            state[slot] = got * take + state[slot] * keep
        low_index = low_index + bit * span
        span *= 2.0
    between = span - 1.0 - low_index if reverse else low_index
    early, later = (1, 0) if reverse else (0, 1)
    reach[later] += state[early] * decay(between)
    state[0] = state[early] * decay(span) + state[later]
    order = [low_index, low_index + span]
    span *= 2.0
    for number, axis in enumerate(plan.high):
        bit = at[axis].astype(F32)
        late = 1.0 - bit if reverse else bit
        high_buf[2 * number] = state[0].astype(BF)
        copy = remote(high_buf.at[2 * number], high_buf.at[2 * number + 1], sends, receives, index, {axis: 1 - at[axis]})
        copy.start()
        copies.append(copy)
        index += 1
        yield
        copy.wait_recv()
        step_decay = decay(span)
        take, keep = late * step_decay + (1.0 - late), late + (1.0 - late) * step_decay
        got = high_buf[2 * number + 1].astype(F32)
        for slot in range(2):
            between = span - 1.0 - order[slot] if reverse else order[slot]
            reach[slot] += got * (late * decay(between))
            order[slot] = order[slot] + bit * span
        state[0] = got * take + state[0] * keep
        span *= 2.0
    for copy in copies:
        copy.wait_send()


def carry_buffers(plan, key_size, value_size):
    return [
        pltpu.VMEM((2, key_size, value_size), F32),
        pltpu.VMEM((2, key_size, value_size), F32),
        pltpu.VMEM((2 * max(len(plan.low), 1), 2, key_size, value_size), BF),
        pltpu.VMEM((2 * max(len(plan.high), 1), key_size, value_size), BF),
    ]


def spread_steps(sq, block, full, sends, receives, base, local_sem):
    rows, width = block.shape
    half = rows // 2
    p, y, c = sq.p, sq.y, sq.c
    top, low = (0, half), (half, half)

    def place(p_, y_, c_, start, count):
        return full.at[p_, pl.ds(start, count), pl.ds(pl.multiple_of((y_ * 2 + c_) * width, width), width)]

    def own(part):
        return block.at[pl.ds(part[0], part[1]), :]

    def send(index, source, target, device):
        copy = remote(source, target, sends, receives, base + index, device)
        copy.start()
        return copy

    def relay(index, p_, y_, part, device):
        return send(index, place(p_, y_, c, *part), place(p_, y_, c, *part), device)

    k0 = send(0, own(top), place(p, y, c, *top), sq.S)
    k2 = send(2, own(low), place(p, y, c, *low), sq.Y)
    k6 = send(6, block, place(p, y, c, 0, rows), sq.C)
    k1 = send(1, own(low), place(p, y, c, *low), sq.S)
    k3 = send(3, own(top), place(p, y, c, *top), sq.Y)
    keep = pltpu.make_async_copy(block, place(p, y, c, 0, rows), local_sem)
    keep.start()
    yield
    k2.wait_recv()
    k4 = relay(4, p, 1 - y, low, sq.S)
    k9 = relay(9, p, 1 - y, low, sq.C)
    k0.wait_recv()
    k5 = relay(5, 1 - p, y, top, sq.Y)
    k7 = relay(7, 1 - p, y, top, sq.C)
    yield
    k1.wait_recv()
    k8 = relay(8, 1 - p, y, low, sq.C)
    k3.wait_recv()
    k10 = relay(10, p, 1 - y, top, sq.C)
    yield
    k5.wait_recv()
    k11 = relay(11, 1 - p, 1 - y, top, sq.C)
    k4.wait_recv()
    k12 = relay(12, 1 - p, 1 - y, low, sq.C)
    for copy in (k6, k7, k8, k9, k10, k11, k12):
        copy.wait_recv()
    for copy in (k0, k1, k2, k3, k4, k5, k6, k7, k8, k9, k10, k11, k12):
        copy.wait_send()
    keep.wait()


def pass_steps(sq, block, full, sends, receives, base, wide):
    rows = full.shape[1]
    width = full.shape[2] // 4
    half = rows // 2
    p, y, c = sq.p, sq.y, sq.c
    parts = ((0, half), (half, half))
    copies = []

    def place(p_, y_, part):
        columns = pl.ds(pl.multiple_of((y_ * 2 + c) * width, width), width)
        return full.at[p_, pl.ds(part[0], part[1]), columns]

    def send(index, source, p_, y_, part, device):
        copy = remote(source, place(p_, y_, part), sends, receives, base + index, device)
        copy.start()
        copies.append(copy)
        return copy

    def own(part):
        return block.at[pl.ds(part[0], part[1]), :]

    far = [send(i, own(part), p, y, part, sq.S) for i, part in enumerate(parts)]
    beside, near = [], []
    if wide:
        beside += [send(2 + i, own(part), p, y, part, sq.Y) for i, part in enumerate(parts)]
        near += [send(4 + i, own(part), p, y, part, sq.C) for i, part in enumerate(parts)]
    yield
    other = []
    for i, part in enumerate(parts):
        far[i].wait_recv()
        other.append(send(6 + i, place(1 - p, y, part), 1 - p, y, part, sq.Y))
        near.append(send(8 + i, place(1 - p, y, part), 1 - p, y, part, sq.C))
    yield
    for i, part in enumerate(parts):
        if wide:
            beside[i].wait_recv()
            near.append(send(10 + i, place(p, 1 - y, part), p, 1 - y, part, sq.C))
        other[i].wait_recv()
        near.append(send(12 + i, place(1 - p, 1 - y, part), 1 - p, 1 - y, part, sq.C))
    yield
    for copy in near:
        copy.wait_recv()
    for copy in copies:
        copy.wait_send()


PASS_COPIES = 14


def reduce_steps(sq, block_of, result, hand, near, total, arrived, sends, receives, base):
    rows, width = result.shape
    half = rows // 2
    p, y, c = sq.p, sq.y, sq.c
    top, low = pl.ds(0, half), pl.ds(half, half)

    def send(index, source, target, device):
        copy = remote(source, target, sends, receives, base + index, device)
        copy.start()
        return copy

    order = ((1 - p, 1 - y), (1 - p, y), (p, 1 - y), (p, y))

    def give(i, p_, y_):
        return remote(hand.at[p_, y_], near.at[p_, y_], sends, receives, base + i, sq.C)

    @pl.loop(0, 4)
    def _(i):
        p_, y_ = (1 - p + i // 2) % 2, (1 - y + i % 2) % 2
        hand[p_, y_] = block_of(p_, y_, 1 - c).astype(BF)
        give(i, p_, y_).start()

    given = [give(i, p_, y_) for i, (p_, y_) in enumerate(order)]

    def join(i):
        p_, y_ = order[i]
        own = block_of(p_, y_, c)
        given[i].wait_recv()
        return own + near[p_, y_].astype(F32)

    total[1 - p, 1 - y] = join(0).astype(BF)
    a = send(4, total.at[1 - p, 1 - y, low], arrived.at[0], sq.S)
    b = send(5, total.at[1 - p, 1 - y, top], arrived.at[1], sq.Y)

    @pl.loop(0, 2)
    def _(i):
        p_, y_ = (1 - p + i) % 2, (y + i) % 2
        own = block_of(p_, y_, c)
        give(1 + i, p_, y_).wait_recv()
        total[p_, y_] = (own + near[p_, y_].astype(F32)).astype(BF)

    e = send(6, total.at[1 - p, y, low], arrived.at[2], sq.S)
    f = send(7, total.at[p, 1 - y, top], arrived.at[3], sq.Y)
    result[...] = join(3)
    yield
    b.wait_recv()
    total[1 - p, y, top] = (total[1 - p, y, top].astype(F32) + arrived[1].astype(F32)).astype(BF)
    g = send(8, total.at[1 - p, y, top], arrived.at[4], sq.S)
    a.wait_recv()
    total[p, 1 - y, low] = (total[p, 1 - y, low].astype(F32) + arrived[0].astype(F32)).astype(BF)
    d = send(9, total.at[p, 1 - y, low], arrived.at[5], sq.Y)
    yield
    e.wait_recv()
    f.wait_recv()
    g.wait_recv()
    result[top, :] += arrived[4].astype(F32) + arrived[3].astype(F32)
    d.wait_recv()
    result[low, :] += arrived[2].astype(F32) + arrived[5].astype(F32)
    for copy in given + [a, b, e, f, g, d]:
        copy.wait_send()


def reduce_room(rows, width):
    return [pltpu.VMEM((2, 2, rows, width), BF)] * 3 + [pltpu.VMEM((6, rows // 2, width), BF)]


def flipped(plan, at, mask):
    return {axis: 1 - at[axis] for i, axis in enumerate(plan.seq) if mask >> i & 1}


def greet_all(plan, at, sq):
    barrier = pltpu.get_barrier_semaphore()
    peers = [flipped(plan, at, mask) for mask in range(1, 1 << len(plan.seq))] + [sq.Y, sq.C, sq.X]
    for peer in peers:
        pl.semaphore_signal(barrier, inc=1, device_id=peer, device_id_type=MESH)
    pl.semaphore_wait(barrier, len(peers))


def column_of(rows, start, sign, rate):
    offset = lax.broadcasted_iota(jnp.int32, (rows, 1), 0).astype(F32)
    return jnp.exp((start + sign * offset) * rate)


def decay_mask(mask, rate):
    rows = mask.shape[0]

    @pl.loop(0, rows // 128)
    def _(i):
        start = pl.multiple_of(i * 128, 128)
        line = lax.broadcasted_iota(jnp.int32, (128, rows), 0) + start
        lane = lax.broadcasted_iota(jnp.int32, (128, rows), 1)
        distance = (line - lane).astype(F32)
        mask[pl.ds(start, 128), :] = jnp.where(distance >= 0, jnp.exp(jnp.maximum(distance, 0.0) * rate), 0.0)


TILE = 256


def row_tiles(full, body):
    rows = full.shape[1]
    each = rows // TILE

    @pl.loop(0, 2 * each)
    def _(i):
        body(i // each, pl.multiple_of(i % each * TILE, TILE), pl.multiple_of(i * TILE, TILE))


def turned(r, slot, start):
    base = r.turn[slot]
    cos_at, sin_at = base[0:1], base[1:2]
    cos_off, sin_off = r.cos_off[pl.ds(start, TILE), :], r.sin_off[pl.ds(start, TILE), :]
    return cos_at * cos_off - sin_at * sin_off, sin_at * cos_off + cos_at * sin_off


def front_kernel(plan, names, *refs):
    r = types.SimpleNamespace(**dict(zip(names, refs)))
    at = {axis: lax.axis_index(axis) for axis in plan.seq + plan.head}
    sq = Square(plan.pair)
    length, model = r.inputs.shape
    width = r.block.shape[1]
    mine = sq.y * 2 + sq.c
    column = pl.multiple_of(mine * width, width)
    rate = r.rate[0:1, 0:1]
    weights = [r.wq, r.wk, r.wv, r.wg, r.wo, r.wu, r.wd]
    key_size, value_size = r.wq.shape[1], r.wv.shape[1]
    saved = []

    def save(source, target):
        copy = pltpu.make_async_copy(source, target, r.save_sem.at[len(saved)])
        copy.start()
        saved.append(copy)

    greet_all(plan, at, sq)
    flip = r.so.shape[0] != r.sq.shape[0]
    outer_shards = [r.so_t, r.sd_t] if flip else [r.so, r.sd]
    shards = [r.sq, r.sk, r.sv, r.sg, outer_shards[0], r.su, outer_shards[1]]
    bulk = Bulk(plan, at, shards, weights, r.bulk_send, r.bulk_receive, r.bulk_local)
    QUERY, KEY, VALUE, GATE, OUT, UP, DOWN = range(7)
    pair, high, low = [bulk.axes[0]], bulk.high, bulk.low

    for row, vector in enumerate((r.gain_one, r.bias_one, r.gain_two, r.bias_two)):
        r.vec[row : row + 1, :] = vector[...].astype(F32)
    r.vec[4:8, :] = jnp.zeros((4, r.vec.shape[1]), F32)
    size = 1 << len(plan.seq)
    copies = []
    for mask in range(1, size):
        copy = remote(r.vec, r.vecs.at[bulk.me], r.vec_send, r.vec_receive, mask, flipped(plan, at, mask))
        copy.start()
        copies.append(copy)
    r.vecs[bulk.me] = r.vec[...]
    bulk.begin(QUERY, bulk.axes)
    bulk.begin(KEY, bulk.axes)
    if flip:
        r.so_t[...] = r.so[...].T
        r.sd_t[...] = r.sd[...].T
    r.cot_bf[...] = r.cot[...].astype(BF)
    for unit in (VALUE, GATE, OUT):
        bulk.begin(unit, low)

    for copy in copies:
        copy.wait_recv()
    step = r.vec.shape[1]
    for j in range(size):
        r.all_gains[:, j * step : (j + 1) * step] = r.vecs[j]
    r.gains[...] = r.all_gains[:, pl.ds(column, width)]

    @pl.loop(0, length // 128)
    def _(i):
        rows = pl.ds(pl.multiple_of(i * 128, 128), 128)
        stream = r.inputs[rows, :]
        mean = jnp.mean(stream, axis=1, keepdims=True)
        inverse = lax.rsqrt(jnp.mean(jnp.square(stream - mean), axis=1, keepdims=True) + EPSILON)
        r.inverse_one[rows, :] = jnp.broadcast_to(inverse, (128, 128))
        normed = (stream - mean) * inverse
        hidden = (normed * r.all_gains[0:1, :] + r.all_gains[1:2, :]).astype(BF)
        r.hidden[sq.p, rows, :] = hidden
        own = (r.inputs[rows, pl.ds(column, width)] - mean) * inverse
        r.normed_one[rows, :] = own
        r.block[rows, :] = (own * r.gains[0:1, :] + r.gains[1:2, :]).astype(BF)

    gains = r.gains[...]
    hid = pass_steps(sq, r.block, r.hidden, r.hid_send, r.hid_receive, 0, False)
    cot = pass_steps(sq, r.cot_bf, r.cot_out, r.cot_send, r.cot_receive, 0, True)
    keep_cot = pltpu.make_async_copy(r.cot_bf, r.cot_out.at[sq.p, :, pl.ds(column, width)], r.local_sem.at[0])
    keep_cot.start()
    next(hid)
    bulk.begin(VALUE, pair + high)
    bulk.paired(QUERY)
    bulk.paired(KEY)
    bulk.first(QUERY)
    bulk.first(KEY)
    bulk.paired(VALUE)
    bulk.begin(GATE, pair + high)
    bulk.begin(OUT, pair + high)
    next(hid)
    decay_mask(r.mask, rate)
    bulk.second(QUERY)
    bulk.second(KEY)
    bulk.first(VALUE)
    next(hid)
    next(hid, None)
    save(r.hidden, r.hidden_out)

    bulk.finish(QUERY)
    bulk.finish(KEY)
    save(r.wq, r.wq_out)
    save(r.wk, r.wk_out)

    def project_keys(slot, start, row):
        hidden = r.hidden[slot, pl.ds(start, TILE), :]
        cosine, sine = turned(r, slot, start)
        for weight, target in ((r.wq, r.q), (r.wk, r.k)):
            value = mm(hidden, weight[...])
            target[pl.ds(row, TILE), :] = rotate(value, cosine, sine).astype(BF)

    row_tiles(r.hidden, project_keys)

    bulk.second(VALUE)
    bulk.paired(GATE)
    bulk.paired(OUT)
    bulk.finish(VALUE)
    save(r.wv, r.wv_out)

    def project_values(slot, start, row):
        r.v[pl.ds(row, TILE), :] = mm(r.hidden[slot, pl.ds(start, TILE), :], r.wv[...]).astype(BF)

    row_tiles(r.hidden, project_values)
    save(r.q, r.q_out)
    save(r.k, r.k_out)
    save(r.v, r.v_out)
    weight_out = column_of(length, float(length), -1.0, rate)
    for slot in range(2):
        rows = slice(slot * length, (slot + 1) * length)
        key = (r.k[rows, :].astype(F32) * weight_out).astype(BF)
        r.state[slot] = t_mm(key, r.v[rows, :])
    carry = carried(
        plan, at, r.state, r.reach, r.low_buf, r.high_buf, rate, length, False, r.carry_send, r.carry_receive, 0
    )
    next(carry)

    def inner(slot, start, row):
        scores = mm_t(r.q[pl.ds(row, TILE), :], r.k[pl.ds(pl.multiple_of(slot * length, length), length), :])
        weights_ = (scores * r.mask[pl.ds(start, TILE), :]).astype(BF)
        r.normed[pl.ds(row, TILE), :] = mm(weights_, r.v[pl.ds(pl.multiple_of(slot * length, length), length), :])

    row_tiles(r.hidden, inner)
    bulk.first(GATE)
    bulk.first(OUT)
    bulk.begin(UP, pair)
    bulk.begin(DOWN, pair)
    next(carry, None)
    bulk.second(GATE)
    bulk.second(OUT)
    bulk.begin(UP, high + low)
    bulk.begin(DOWN, low)
    bulk.finish(GATE)
    save(r.wg, r.wg_out)

    def gates(slot, start, row):
        r.gate[pl.ds(row, TILE), :] = mm(r.hidden[slot, pl.ds(start, TILE), :], r.wg[...])

    row_tiles(r.hidden, gates)
    save(r.gate, r.gate_out)
    bulk.paired(UP, low)
    bulk.paired(DOWN, low)
    for _ in carry:
        pass
    for slot in range(2):
        r.reach_bf[slot] = r.reach[slot].astype(BF)
    save(r.reach_bf, r.reach_out)

    def outer(slot, start, row):
        rows = pl.ds(row, TILE)
        offset = lax.broadcasted_iota(jnp.int32, (TILE, 1), 0) + start
        cross = mm(r.q[rows, :], r.reach_bf[slot]) * jnp.exp(offset.astype(F32) * rate)
        retained = r.normed[rows, :] + cross
        center = retained - jnp.mean(retained, axis=1, keepdims=True)
        inverse = lax.rsqrt(jnp.mean(center * center, axis=1, keepdims=True) + EPSILON)
        value = center * inverse
        r.normed[rows, :] = value
        r.inverse[rows, :] = jnp.broadcast_to(inverse, (TILE, 128))
        gate = r.gate[rows, :]
        r.gated[rows, :] = (gate * jax.nn.sigmoid(gate) * value).astype(BF)

    row_tiles(r.hidden, outer)
    save(r.normed, r.normed_out)
    save(r.inverse, r.inverse_out)
    save(r.gated, r.gated_out)
    bulk.finish(OUT)
    save(r.wo, r.wo_out)

    def out_block(p_, y_, c_):
        rows = pl.ds(pl.multiple_of(p_ * length, length), length)
        return mm_t(r.gated[rows, :], r.wo[pl.ds(pl.multiple_of((y_ * 2 + c_) * width, width), width), :])

    def nothing():
        pass

    def rest_of_up():
        bulk.forward(UP, bulk.bit[pair[0]], high)
        bulk.begin(DOWN, high)

    def rest_of_down():
        bulk.forward(DOWN, bulk.bit[pair[0]], high)
        next(cot)
        bulk.first(UP)

    def second_up():
        bulk.second(UP)
        bulk.first(DOWN)

    reduce = reduce_steps(
        sq, out_block, r.middle, r.hand, r.near, r.total, r.arrived, r.sends, r.receives, SPREAD_COPIES
    )
    together(reduce, nothing, rest_of_up)
    whole = r.middle[...] + r.inputs[:, pl.ds(column, width)]
    r.middle[...] = whole
    mean = jnp.mean(whole, axis=1, keepdims=True)
    deviation = jnp.mean(jnp.square(whole - mean), axis=1, keepdims=True)
    base = SPREAD_COPIES + REDUCE_COPIES
    means, spreads = exchange(sq, mean, deviation, r.stats, r.sends, r.receives, base)
    center = sum(means) * (1.0 / len(means))
    variance = sum(s + jnp.square(m - center) for m, s in zip(means, spreads)) * (1.0 / len(means))
    mean, scale = upright(center, lax.rsqrt(variance + EPSILON))
    r.inverse_two[...] = jnp.broadcast_to(scale, r.inverse_two.shape)
    value = (r.middle[...] - mean) * scale
    r.normed_two[...] = value
    r.block[...] = (value * gains[2:3] + gains[3:4]).astype(BF)
    spread = spread_steps(sq, r.block, r.mid_out, r.sends, r.receives, 0, r.local_sem.at[1])
    together(spread, nothing, rest_of_down, second_up)
    bulk.finish(UP)
    save(r.wu, r.wu_out)
    next(cot)
    bulk.second(DOWN)
    next(cot)
    next(cot, None)
    bulk.finish(DOWN)
    save(r.wd, r.wd_out)
    bulk.drain()
    keep_cot.wait()
    for copy in copies:
        copy.wait_send()
    for copy in saved:
        copy.wait()


def front(plan, shards, inputs, cot, vectors, rate, turn, cos_off, sin_off, number):
    length, model = inputs.shape
    width = cot.shape[1]
    size = 1 << len(plan.seq)
    key_size, value_size, hidden = shards[0].shape[1] // 2, shards[2].shape[1] // 2, shards[5].shape[1] // 2
    any_spec, vmem_spec = pl.BlockSpec(memory_space=pl.ANY), pl.BlockSpec(memory_space=pltpu.VMEM)
    both = 2 * length

    def shape(dims, kind=BF):
        return jax.ShapeDtypeStruct(dims, kind)

    sq, sk, sv, sg, so, su, sd = shards
    rows = sq.shape[0]
    flip = rows % 128 == 0
    if not flip:
        so, sd = so.T, sd.T
    far = dict(sq=sq, sk=sk, sv=sv, sg=sg, su=su)
    near = dict(so=so, sd=sd, inputs=inputs, cot=cot, rate=rate, turn=turn, cos_off=cos_off, sin_off=sin_off)
    gain_one, bias_one, gain_two, bias_two = [v[None] for v in vectors]
    near.update(gain_one=gain_one, bias_one=bias_one, gain_two=gain_two, bias_two=bias_two)
    wq, wk, wv, wg, wu = [(model, s.shape[1] // 2) for s in far.values()]
    wo, wd = (model, value_size), (model, hidden)
    far_outs = dict(
        wq_out=shape(wq),
        wk_out=shape(wk),
        wv_out=shape(wv),
        wg_out=shape(wg),
        wo_out=shape(wo),
        wu_out=shape(wu),
        wd_out=shape(wd),
        hidden_out=shape((2, length, model)),
        cot_out=shape((2, length, model)),
        mid_out=shape((2, length, model)),
        q_out=shape((both, key_size)),
        k_out=shape((both, key_size)),
        v_out=shape((both, value_size)),
        reach_out=shape((2, key_size, value_size)),
        gate_out=shape((both, value_size), F32),
        normed_out=shape((both, value_size), F32),
        inverse_out=shape((both, 128), F32),
        gated_out=shape((both, value_size)),
    )
    near_outs = dict(
        middle=shape((length, width), F32),
        normed_one=shape((length, width), F32),
        inverse_one=shape((length, 128), F32),
        normed_two=shape((length, width), F32),
        inverse_two=shape((length, 128), F32),
        gains=shape((8, width), F32),
    )
    carries = carry_buffers(plan, key_size, value_size)
    count = SPREAD_COPIES + REDUCE_COPIES + 3
    dma = pltpu.SemaphoreType.DMA
    hand, near_room, total, arrived = reduce_room(length, width)
    scratch = dict(
        so_t=pltpu.VMEM((rows, 2 * value_size) if flip else (16, 128), BF),
        sd_t=pltpu.VMEM((rows, 2 * hidden) if flip else (16, 128), BF),
        cot_bf=pltpu.VMEM((length, width), BF),
        wq=pltpu.VMEM(wq, BF),
        wk=pltpu.VMEM(wk, BF),
        wv=pltpu.VMEM(wv, BF),
        wg=pltpu.VMEM(wg, BF),
        wo=pltpu.VMEM(wo, BF),
        wu=pltpu.VMEM(wu, BF),
        wd=pltpu.VMEM(wd, BF),
        hidden=pltpu.VMEM((2, length, model), BF),
        block=pltpu.VMEM((length, width), BF),
        q=pltpu.VMEM((both, key_size), BF),
        k=pltpu.VMEM((both, key_size), BF),
        v=pltpu.VMEM((both, value_size), BF),
        gate=pltpu.VMEM((both, value_size), F32),
        normed=pltpu.VMEM((both, value_size), F32),
        inverse=pltpu.VMEM((both, 128), F32),
        gated=pltpu.VMEM((both, value_size), BF),
        mask=pltpu.VMEM((length, length), F32),
        state=carries[0],
        reach=carries[1],
        low_buf=carries[2],
        high_buf=carries[3],
        reach_bf=pltpu.VMEM((2, key_size, value_size), BF),
        vec=pltpu.VMEM((8, rows), F32),
        vecs=pltpu.VMEM((size, 8, rows), F32),
        stats=pltpu.VMEM((4, 8, length), F32),
        hand=hand,
        near=near_room,
        total=total,
        arrived=arrived,
        bulk_send=dma((7 * size,)),
        bulk_receive=dma((7 * size,)),
        bulk_local=dma((7,)),
        vec_send=dma((size,)),
        vec_receive=dma((size,)),
        carry_send=dma((len(plan.seq),)),
        carry_receive=dma((len(plan.seq),)),
        all_gains=pltpu.VMEM((8, model), F32),
        hid_send=dma((PASS_COPIES,)),
        hid_receive=dma((PASS_COPIES,)),
        cot_send=dma((PASS_COPIES,)),
        cot_receive=dma((PASS_COPIES,)),
        sends=dma((count,)),
        receives=dma((count,)),
        local_sem=dma((3,)),
        save_sem=dma((32,)),
    )
    names = list(far) + list(near) + list(far_outs) + list(near_outs) + list(scratch)
    results = pl.pallas_call(
        functools.partial(front_kernel, plan, names),
        out_shape=tuple(far_outs.values()) + tuple(near_outs.values()),
        in_specs=[any_spec] * len(far) + [vmem_spec] * len(near),
        out_specs=(any_spec,) * len(far_outs) + (vmem_spec,) * len(near_outs),
        scratch_shapes=list(scratch.values()),
        compiler_params=pltpu.CompilerParams(
            collective_id=number, has_side_effects=True, vmem_limit_bytes=VMEM_LIMIT
        ),
        name="front",
    )(*far.values(), *near.values())
    return types.SimpleNamespace(**dict(zip(list(far_outs) + list(near_outs), results)))


SLOT = (1, 0, 2, 0, 3, None)


class Return:
    def __init__(self, plan, at, totals, spare, got, sends, receives):
        self.at, self.totals, self.spare, self.got = at, totals, spare, got
        self.sends, self.receives = sends, receives
        self.order = plan.low + list(reversed(plan.high)) + [plan.pair]
        self.bit = {axis: 1 << i for i, axis in enumerate(plan.seq)}
        self.size = 1 << len(plan.seq)
        self.me = sum(at[axis] * self.bit[axis] for axis in self.order)
        self.copies = {}

    def stage_of(self, mask):
        for stage, axis in enumerate(self.order):
            if mask & self.bit[axis]:
                return stage
        return len(self.order)

    def masks(self, stage):
        found = [m for m in range(1, self.size) if self.stage_of(m) == stage]
        return sorted(found, key=lambda m: (self.stage_of(m ^ self.bit[self.order[stage]]), m))

    def link(self, unit, mask, axis=None):
        axis = axis or self.order[self.stage_of(mask)]
        return remote(
            self.total(unit, mask),
            self.got.at[unit, mask - 1],
            self.sends,
            self.receives,
            unit * self.size + mask,
            {axis: 1 - self.at[axis]},
        )

    def total(self, unit, mask):
        rows, columns = self.got.shape[2:]
        if SLOT[unit] is None:
            across, down = self.spare.shape[2] // columns, self.spare.shape[1] // rows
            tile = self.spare.at[mask // (across * down)]
            return tile.at[pl.ds(mask // across % down * rows, rows), pl.ds(mask % across * columns, columns)]
        return self.totals.at[SLOT[unit], pl.ds(mask * rows, rows), :]

    def send(self, unit, mask):
        copy = self.link(unit, mask)
        copy.start()
        self.copies[unit, mask] = copy

    def made(self, unit, mask):
        if self.stage_of(mask) == 0:
            self.send(unit, mask)

    def ahead(self, stage):
        bit = self.bit[self.order[stage]]
        masks = self.masks(stage)
        first = [m for m in masks if m ^ bit and self.stage_of(m ^ bit) == stage + 1]
        return first, [m for m in masks if m not in first]

    def collect(self, unit, stage, masks):
        axis = self.order[stage]
        for mask in masks:
            target = mask ^ self.bit[axis]
            self.link(unit, mask).wait_recv()
            total, got = self.total(unit, target), self.got.at[unit, mask - 1]

            @pl.loop(0, total.shape[0] // 64)
            def _(i, total=total, got=got):
                rows = pl.ds(pl.multiple_of(i * 64, 64), 64)
                total[rows, :] = (total[rows, :].astype(F32) + got[rows, :].astype(F32)).astype(BF)

            if self.stage_of(target) == stage + 1 and target:
                self.send(unit, target)

    def early(self, unit):
        self.collect(unit, 0, self.ahead(0)[0])

    def late(self, unit):
        self.collect(unit, 0, self.ahead(0)[1])

    def middle(self, unit):
        for stage in range(1, len(self.order) - 1):
            self.collect(unit, stage, self.masks(stage))

    def last(self, unit):
        return self.got.at[unit, self.bit[self.order[-1]] - 1]

    def last_arrived(self, unit):
        self.link(unit, self.bit[self.order[-1]]).wait_recv()

    def clear(self, unit):
        for (number, _), copy in self.copies.items():
            if number == unit:
                copy.wait_send()


def back_kernel(plan, names, *refs):
    r = types.SimpleNamespace(**dict(zip(names, refs)))
    at = {axis: lax.axis_index(axis) for axis in plan.seq + plan.head}
    sq = Square(plan.pair)
    length, width = r.cot.shape
    key_size, value_size = r.q.shape[1], r.v.shape[1]
    mine = sq.y * 2 + sq.c
    rate = r.rate[0:1, 0:1]
    UP, DOWN, OUT, GATE, VALUE, KEYS = range(6)
    back = Return(plan, at, r.totals, r.tiles, r.got, r.bulk_send, r.bulk_receive)
    piece, model = r.got.shape[2], r.mid.shape[2]
    strip = r.strips.shape[2]
    per_strip = strip // piece

    loads = {}

    def load(name, source, target):
        copy = pltpu.make_async_copy(source, target, r.load_sem.at[len(loads)])
        copy.start()
        loads[name] = copy

    def ready(*wanted):
        for name in wanted:
            loads[name].wait()

    load("wu", r.wu, r.weights.at[0])
    load("wd", r.wd, r.weights.at[1])

    parts = model // value_size

    def tile_copy(source, i):
        each = length // TILE
        rows = source.at[i // each, pl.ds(i % each * TILE, TILE), :]
        return [pltpu.make_async_copy(rows, r.tiles.at[i % 2], r.tile_sem.at[i % 2, 0])]

    def cot_tile(i, part):
        rows = pl.ds(pl.multiple_of((i % 2 * parts + part) * TILE, TILE), TILE)
        return r.totals.at[r.totals.shape[0] - 1, rows, :]

    def cot_copy(i):
        each = length // TILE
        return [
            pltpu.make_async_copy(
                r.cotf.at[i // each, pl.ds(i % each * TILE, TILE), pl.ds(part * value_size, value_size)],
                cot_tile(i, part),
                r.tile_sem.at[i % 2, 1 + part],
            )
            for part in range(parts)
        ]

    def start(copies):
        for copy in copies:
            copy.start()

    def wait(copies):
        for copy in copies:
            copy.wait()

    tile_count = 2 * length // TILE
    start(tile_copy(r.mid, 0) + cot_copy(0))
    greet_all(plan, at, sq)
    load("wo", r.wo, r.weights.at[2])
    load("gated", r.gated_in, r.gated)
    load("gate", r.gate_in, r.gate)
    load("normed", r.normed_in, r.normed)
    load("inverse", r.inverse_in, r.inverse)
    load("q", r.q_in, r.q)
    load("k", r.k_in, r.k)
    load("v", r.v_in, r.v)
    load("reach", r.reach_in, r.in_bf)
    load("middle", r.middle_in, r.layer_out)
    ready("wu", "wd")

    @pl.loop(0, tile_count)
    def _(i):
        @pl.when(i + 1 < tile_count)
        def _():
            start(tile_copy(r.mid, i + 1) + cot_copy(i + 1))

        wait(tile_copy(r.mid, i) + cot_copy(i))
        rows = pl.ds(pl.multiple_of(i * TILE, TILE), TILE)
        preact = mm(r.tiles[i % 2], r.weights[0])
        cdf = 0.5 * (1.0 + lax.erf(preact * 0.7071067811865476))
        slope = cdf + preact * (jnp.exp(-0.5 * preact * preact) * 0.3989422804014327)
        r.hidden_ff[rows, :] = (preact * cdf).astype(BF)
        grad = sum(
            mm(cot_tile(i, part)[...], r.weights[1, part * value_size : (part + 1) * value_size, :])
            for part in range(parts)
        )
        r.grad_pre[rows, :] = (grad * slope).astype(BF)

    def strip_copy(source, mask, number):
        start = pl.multiple_of((back.me ^ mask) // per_strip * strip, strip)
        half = r.strips.at[number % 2]
        return [
            pltpu.make_async_copy(
                source.at[slot, :, pl.ds(start, strip)],
                half.at[pl.ds(slot * length, length), :],
                r.strip_sem.at[number % 2, slot],
            )
            for slot in range(2)
        ]

    def produce(unit, source, grads, masks):
        count = len(masks)
        step = masks[1] - masks[0] if count > 1 else 0
        even = all(mask == masks[0] + number * step for number, mask in enumerate(masks))

        def one(number, mask):
            for copy in strip_copy(source, mask, number):
                copy.wait()
            value = t_mm(r.strips[number % 2], grads[...])
            if per_strip > 1:
                r.whole_strip[...] = value
                inside = pl.multiple_of((back.me ^ mask) % per_strip * piece, piece)
                value = r.whole_strip[pl.ds(inside, piece), :]
            back.total(unit, mask)[...] = value.astype(BF)

        for copy in strip_copy(source, masks[0], 0):
            copy.start()
        if even:

            @pl.loop(0, count)
            def _(number):
                @pl.when(number + 1 < count)
                def _():
                    for copy in strip_copy(source, masks[0] + (number + 1) * step, number + 1):
                        copy.start()

                mask = masks[0] + number * step
                one(number, mask)
                if back.stage_of(masks[0]) == 0:
                    back.link(unit, mask, back.order[0]).start()

            for mask in masks:
                if back.stage_of(mask) == 0:
                    back.copies[unit, mask] = back.link(unit, mask)
        else:
            for number, mask in enumerate(masks):
                if number + 1 < count:
                    for copy in strip_copy(source, masks[number + 1], number + 1):
                        copy.start()
                one(number, mask)
                back.made(unit, mask)

    away_first, away_rest = back.ahead(0)
    low_bit = back.bit[back.order[0]]
    home_first, home_rest = ([m ^ low_bit for m in masks] for masks in (away_first, away_rest))

    def blocks(grads, weight):
        def block_of(p_, y_, c_):
            rows = pl.ds(pl.multiple_of(p_ * length, length), length)
            columns = pl.ds(pl.multiple_of((y_ * 2 + c_) * width, width), width)
            return sum(mm_t(g[rows, :], r.weights[w, columns, :]) for g, w in zip(grads, weight))

        return block_of

    def reduce(grads, weight, result, base):
        return reduce_steps(
            sq, blocks(grads, weight), result, r.hand, r.near, r.near, r.arrived, r.sends, r.receives, base
        )

    emitted = {}

    def emit(unit):
        own = at[plan.pair]
        back.last_arrived(unit)
        emitted[unit] = [
            pltpu.make_async_copy(source, r.halves.at[unit, half], r.emit_sem.at[unit, number])
            for number, (half, source) in enumerate(((own, back.total(unit, 0)), (1 - own, back.last(unit))))
        ]
        start(emitted[unit])

    def clear(unit):
        back.clear(unit)
        wait(emitted[unit])

    def norm_sums(upstream, gain, normed, inverse, base_stream, result, row, stats, base):
        value = upstream[...]
        product = value * normed[...]
        r.sums[row : row + 1, :] = jnp.sum(product, axis=0, keepdims=True)
        r.sums[row + 1 : row + 2, :] = jnp.sum(value, axis=0, keepdims=True)
        first = jnp.mean(value * gain, axis=1, keepdims=True)
        second = jnp.mean(product * gain, axis=1, keepdims=True)
        firsts, seconds = exchange(sq, first, second, stats, r.sends, r.receives, base)
        share = 1.0 / len(firsts)
        first, second = upright(sum(firsts) * share, sum(seconds) * share)
        result[...] = base_stream[...] + inverse[:, 0:1] * (upstream[...] * gain - first - normed[...] * second)

    def down_last():
        produce(DOWN, r.cotf, r.hidden_ff, away_rest)
        produce(DOWN, r.cotf, r.hidden_ff, home_first)
        produce(UP, r.mid, r.grad_pre, away_first)

    base = SPREAD_COPIES
    together(
        reduce([r.grad_pre], [0], r.upstream, base),
        lambda: produce(DOWN, r.cotf, r.hidden_ff, away_first),
        down_last,
    )
    base += REDUCE_COPIES
    back.early(DOWN)
    load("wv", r.wv, r.weights.at[0])
    norm_sums(r.upstream, r.gains[2:3, :], r.normed_two, r.inverse_two, r.cot, r.grad_middle, 2, r.stats, base)
    base += 3
    block = r.hand.at[0, 0]
    block[...] = r.grad_middle[...].astype(BF)

    def up_next():
        produce(UP, r.mid, r.grad_pre, away_rest)
        produce(DOWN, r.cotf, r.hidden_ff, home_rest)

    def up_last():
        back.late(DOWN)
        produce(UP, r.mid, r.grad_pre, home_rest)

    together(
        spread_steps(sq, block, r.gmid, r.sends, r.receives, 0, r.local_sem.at[0]),
        up_next,
        lambda: produce(UP, r.mid, r.grad_pre, home_first),
    )
    up_last()
    ready("wo", "gated", "gate", "normed", "inverse")
    back.early(UP)

    start(tile_copy(r.gmid, 0))
    @pl.loop(0, tile_count)
    def _(i):
        @pl.when(i + 1 < tile_count)
        def _():
            start(tile_copy(r.gmid, i + 1))

        wait(tile_copy(r.gmid, i))
        rows = pl.ds(pl.multiple_of(i * TILE, TILE), TILE)
        grad = mm(r.tiles[i % 2], r.weights[2])
        gate = r.gate[rows, :]
        normed = r.normed[rows, :]
        logistic = jax.nn.sigmoid(gate)
        swish = gate * logistic
        r.grad_gate[rows, :] = (grad * normed * (logistic + swish * (1.0 - logistic))).astype(BF)
        scaled = grad * swish
        r.grad_mixed[rows, :] = (
            r.inverse[rows, 0:1]
            * (
                scaled
                - jnp.mean(scaled, axis=1, keepdims=True)
                - normed * jnp.mean(scaled * normed, axis=1, keepdims=True)
            )
        ).astype(BF)
    load("wg", r.wg, r.weights.at[2])
    back.middle(DOWN)

    ready("q", "k", "v", "reach")
    decay_mask(r.mask, rate)
    weight_out = column_of(length, 1.0, 1.0, rate)
    for slot in range(2):
        rows = slice(slot * length, (slot + 1) * length)
        query = (r.q[rows, :].astype(F32) * weight_out).astype(BF)
        r.state[slot] = t_mm(query, r.grad_mixed[rows, :])
    carry = carried(
        plan, at, r.state, r.reach, r.low_buf, r.high_buf, rate, length, True, r.carry_send, r.carry_receive, 0
    )
    next(carry)
    produce(OUT, r.gmid, r.gated, away_first)
    weight_in = column_of(length, 0.0, 1.0, rate)
    weight_back = column_of(length, length - 1.0, -1.0, rate)

    def rotated_back(value, slot):
        base_ = r.turn[slot]
        cosine = base_[0:1] * r.cos_off[...] - base_[1:2] * r.sin_off[...]
        sine = base_[1:2] * r.cos_off[...] + base_[0:1] * r.sin_off[...]
        return unrotate(value, cosine, sine)

    @pl.loop(0, 2)
    def _(slot):
        rows = pl.ds(pl.multiple_of(slot * length, length), length)
        weights = (mm_t(r.grad_mixed[rows, :], r.v[rows, :]) * r.mask[...]).astype(BF)
        value = mm(weights, r.k[rows, :]) + mm_t(r.grad_mixed[rows, :], r.in_bf[slot]) * weight_in
        r.grad_keys[rows, 0:key_size] = rotated_back(value, slot).astype(BF)
        r.gate[rows, 0:key_size] = t_mm(weights, r.q[rows, :])
        weights = (mm_t(r.q[rows, :], r.k[rows, :]) * r.mask[...]).astype(BF)
        r.normed[rows, :] = t_mm(weights, r.grad_mixed[rows, :])

    produce(OUT, r.gmid, r.gated, away_rest)
    next(carry, None)
    feed = reduce([r.hidden_ff], [1], r.grad_inputs, base)
    base += REDUCE_COPIES
    next(feed)
    load("wk", r.wk, r.weights.at[1, :, pl.ds(key_size, key_size)])
    load("wq", r.wq, r.weights.at[1, :, pl.ds(0, key_size)])
    emit(DOWN)
    clear(DOWN)
    produce(GATE, r.hid, r.grad_gate, away_first)
    produce(OUT, r.gmid, r.gated, home_first)
    back.early(OUT)
    next(feed)
    produce(GATE, r.hid, r.grad_gate, away_rest)
    back.late(UP)
    for _ in carry:
        pass
    out_bf = r.low_buf.at[0]
    for slot in range(2):
        out_bf[slot] = r.reach[slot].astype(BF)

    @pl.loop(0, 2)
    def _(slot):
        rows = pl.ds(pl.multiple_of(slot * length, length), length)
        value = r.gate[rows, 0:key_size] + mm_t(r.v[rows, :], out_bf[slot]) * weight_back
        r.grad_keys[rows, key_size : 2 * key_size] = rotated_back(value, slot).astype(BF)
        value = r.normed[rows, :] + mm(r.k[rows, :], out_bf[slot]) * weight_back
        r.grad_pre[rows, :] = value.astype(BF)

    produce(VALUE, r.hid, r.grad_pre, away_first)
    produce(KEYS, r.hid, r.grad_keys, away_first)
    produce(VALUE, r.hid, r.grad_pre, away_rest)
    produce(KEYS, r.hid, r.grad_keys, away_rest)
    for _ in feed:
        pass
    normed_one = r.gate.at[pl.ds(0, length), :]
    load("normed_one", r.normed_one_in, normed_one)
    peers = (sq.S, sq.Y, sq.C)
    for number, peer in enumerate(peers):
        pl.semaphore_signal(r.again.at[number], inc=1, device_id=peer, device_id_type=MESH)
    ready("middle")
    r.layer_out[...] += r.grad_inputs[...]
    back.middle(UP)
    produce(GATE, r.hid, r.grad_gate, home_first)
    back.early(GATE)
    produce(OUT, r.gmid, r.gated, home_rest)
    back.late(OUT)
    back.middle(OUT)
    for number in range(len(peers)):
        pl.semaphore_wait(r.again.at[number], 1)

    ready("wv", "wg", "wk", "wq", "normed_one")

    def value_next():
        produce(VALUE, r.hid, r.grad_pre, home_first)
        back.early(VALUE)
        produce(KEYS, r.hid, r.grad_keys, home_first)

    def keys_next():
        back.early(KEYS)
        produce(GATE, r.hid, r.grad_gate, home_rest)
        back.late(GATE)
        back.middle(GATE)

    together(
        reduce([r.grad_keys, r.grad_pre, r.grad_gate], [1, 0, 2], r.upstream, base),
        value_next,
        keys_next,
    )
    base += REDUCE_COPIES
    norm_sums(r.upstream, r.gains[0:1, :], normed_one, r.inverse_one, r.grad_middle, r.grad_inputs, 0, r.stats_two, base)
    base += 3

    copies = []
    r.all_sums[back.me] = r.sums[...]
    for mask in range(1, back.size):
        copy = remote(r.sums, r.all_sums.at[back.me], r.sum_send, r.sum_receive, mask, flipped(plan, at, mask))
        copy.start()
        copies.append(copy)
    produce(VALUE, r.hid, r.grad_pre, home_rest)
    produce(KEYS, r.hid, r.grad_keys, home_rest)
    back.late(VALUE)
    back.late(KEYS)
    emit(UP)
    back.middle(VALUE)
    emit(OUT)
    back.middle(KEYS)
    emit(GATE)
    for copy in copies:
        copy.wait_recv()
    total = r.all_sums[0]
    for i in range(1, back.size):
        total = total + r.all_sums[i]
    r.by_block[mine] = total
    for index, device in enumerate((sq.Y, sq.C, sq.X)):
        copy = remote(r.by_block.at[mine], r.by_block.at[mine], r.sends, r.receives, base + index, device)
        copy.start()
        copies.append(copy)
    for copy in copies[-3:]:
        copy.wait_recv()
    r.sums_out[...] = r.by_block[back.me * piece // width]
    for copy in copies:
        copy.wait_send()
    emit(VALUE)
    emit(KEYS)
    for unit in (UP, OUT, GATE, VALUE, KEYS):
        clear(unit)


def back_pass(plan, f, cot, rate, turn, cos_off, sin_off, rows, number):
    length, width = cot.shape
    size = 1 << len(plan.seq)
    model = f.wq_out.shape[0]
    key_size, value_size = f.q_out.shape[1], f.v_out.shape[1]
    hidden = f.wu_out.shape[1]
    both = 2 * length
    any_spec, vmem_spec = pl.BlockSpec(memory_space=pl.ANY), pl.BlockSpec(memory_space=pltpu.VMEM)

    def shape(dims, kind=F32):
        return jax.ShapeDtypeStruct(dims, kind)

    far = dict(
        wq=f.wq_out,
        wk=f.wk_out,
        wv=f.wv_out,
        wg=f.wg_out,
        wo=f.wo_out,
        wu=f.wu_out,
        wd=f.wd_out,
        hid=f.hidden_out,
        mid=f.mid_out,
        cotf=f.cot_out,
        q_in=f.q_out,
        k_in=f.k_out,
        v_in=f.v_out,
        reach_in=f.reach_out,
        gate_in=f.gate_out,
        normed_in=f.normed_out,
        inverse_in=f.inverse_out,
        gated_in=f.gated_out,
        middle_in=f.middle,
        normed_one_in=f.normed_one,
    )
    near = dict(
        cot=cot,
        inverse_one=f.inverse_one,
        normed_two=f.normed_two,
        inverse_two=f.inverse_two,
        gains=f.gains,
        rate=rate,
        turn=turn,
        cos_off=cos_off,
        sin_off=sin_off,
    )
    far_outs = dict(halves=shape((6, 2, rows, value_size), BF), gmid=shape((2, length, model), BF))
    near_outs = dict(
        layer_out=shape((length, width)), grad_inputs=shape((length, width)), sums_out=shape((8, width))
    )
    carries = carry_buffers(plan, key_size, value_size)
    dma = pltpu.SemaphoreType.DMA
    count = SPREAD_COPIES + 3 * REDUCE_COPIES + 9
    strip = max(rows, 128)
    hand, near_room, _, arrived = reduce_room(length, width)
    scratch = dict(
        weights=pltpu.VMEM((3, model, value_size), BF),
        tiles=pltpu.VMEM((2, TILE, model), BF),
        strips=pltpu.VMEM((2, both, strip), BF),
        q=pltpu.VMEM((both, key_size), BF),
        k=pltpu.VMEM((both, key_size), BF),
        v=pltpu.VMEM((both, value_size), BF),
        gate=pltpu.VMEM((both, value_size), F32),
        normed=pltpu.VMEM((both, value_size), F32),
        inverse=pltpu.VMEM((both, 128), F32),
        gated=pltpu.VMEM((both, value_size), BF),
        in_bf=pltpu.VMEM((2, key_size, value_size), BF),
        mask=pltpu.VMEM((length, length), F32),
        state=carries[0],
        reach=carries[1],
        low_buf=carries[2],
        high_buf=carries[3],
        hidden_ff=pltpu.VMEM((both, hidden), BF),
        grad_pre=pltpu.VMEM((both, hidden), BF),
        grad_gate=pltpu.VMEM((both, value_size), BF),
        grad_mixed=pltpu.VMEM((both, value_size), BF),
        grad_keys=pltpu.VMEM((both, 2 * key_size), BF),
        upstream=pltpu.VMEM((length, width), F32),
        grad_middle=pltpu.VMEM((length, width), F32),
        hand=hand,
        near=near_room,
        arrived=arrived,
        totals=pltpu.VMEM((4, model, value_size), BF),
        got=pltpu.VMEM((6, size - 1, rows, value_size), BF),
        stats=pltpu.VMEM((4, 8, length), F32),
        stats_two=pltpu.VMEM((4, 8, length), F32),
        sums=pltpu.VMEM((8, width), F32),
        all_sums=pltpu.VMEM((size, 8, width), F32),
        by_block=pltpu.VMEM((4, 8, width), F32),
        whole_strip=pltpu.VMEM((strip, value_size) if strip > rows else (8, 128), F32),
        bulk_send=dma((6 * size,)),
        bulk_receive=dma((6 * size,)),
        load_sem=dma((24,)),
        tile_sem=dma((2, 1 + model // value_size)),
        strip_sem=dma((2, 2)),
        emit_sem=dma((6, 2)),
        carry_send=dma((len(plan.seq),)),
        carry_receive=dma((len(plan.seq),)),
        sum_send=dma((size,)),
        sum_receive=dma((size,)),
        sends=dma((count,)),
        receives=dma((count,)),
        local_sem=dma((1,)),
        again=pltpu.SemaphoreType.REGULAR((3,)),
    )
    names = list(far) + list(near) + list(far_outs) + list(near_outs) + list(scratch)

    def kernel(*refs):
        back_kernel(plan, names, *refs)

    results = pl.pallas_call(
        kernel,
        out_shape=tuple(far_outs.values()) + tuple(near_outs.values()),
        in_specs=[any_spec] * len(far) + [vmem_spec] * len(near),
        out_specs=(any_spec,) * len(far_outs) + (vmem_spec,) * len(near_outs),
        scratch_shapes=list(scratch.values()),
        compiler_params=pltpu.CompilerParams(
            collective_id=number, has_side_effects=True, vmem_limit_bytes=VMEM_LIMIT
        ),
        name="back",
    )(*far.values(), *near.values())
    out = types.SimpleNamespace(**dict(zip(list(far_outs) + list(near_outs), results)))
    return finish(out, key_size)


def finish_kernel(key_size, halves, layer_in, grad_in, *refs):
    *outs, layer_out, grad_out = refs[:9]
    *stages, layer, grad, sems = refs[9:]
    loads = [
        pltpu.make_async_copy(source, stage, sems.at[number])
        for number, (source, stage) in enumerate(((layer_in, layer), (grad_in, grad)))
    ]
    for copy in loads:
        copy.start()
    stores = []

    def store(stage, target):
        copy = pltpu.make_async_copy(stage, target, sems.at[2 + len(stores)])
        copy.start()
        stores.append(copy)

    rows, columns = halves.shape[2:]
    for out, stage, unit, first, width in zip(
        outs, stages, (5, 5, 4, 3, 0, 2, 1), (0, key_size, 0, 0, 0, 0, 0), (key_size,) * 2 + (columns,) * 5
    ):
        for half in range(2):
            value = halves[unit, half, :, first : first + width].astype(F32)
            if out.shape[0] == rows:
                stage[:, half * width : (half + 1) * width] = value
            else:
                stage[half * width : (half + 1) * width, :] = value.T
        store(stage, out)
    for copy, stage, out in zip(loads, (layer, grad), (layer_out, grad_out)):
        copy.wait()
        store(stage, out)
    for copy in stores:
        copy.wait()


def finish(b, key_size):
    rows, value_size = b.halves.shape[2:]
    turned = rows % 128 == 0
    flat = [(rows, 2 * w) for w in (key_size, key_size, value_size, value_size, value_size)]
    shapes = flat + [(2 * value_size, rows) if turned else (rows, 2 * value_size)] * 2 + [b.layer_out.shape] * 2
    any_spec = pl.BlockSpec(memory_space=pl.ANY)
    results = pl.pallas_call(
        functools.partial(finish_kernel, key_size),
        out_shape=tuple(jax.ShapeDtypeStruct(s, F32) for s in shapes),
        in_specs=[pl.BlockSpec(memory_space=pltpu.VMEM), any_spec, any_spec],
        out_specs=tuple([any_spec] * len(shapes)),
        scratch_shapes=[pltpu.VMEM(s, F32) for s in shapes] + [pltpu.SemaphoreType.DMA((2 + len(shapes),))],
        name="finish",
    )(b.halves, b.layer_out, b.grad_inputs)
    gq, gk, gv, gg, gu, go, gd, layer_out, grad_inputs = results
    if not turned:
        go, gd = go.T, gd.T
    return types.SimpleNamespace(
        gq=gq, gk=gk, gv=gv, gg=gg, gu=gu, go=go, gd=gd, layer_out=layer_out, grad_inputs=grad_inputs, sums_out=b.sums_out
    )


def rotate(values, cosine, sine):
    half = values.shape[1] // 2
    first, second = values[:, :half], values[:, half:]
    return jnp.concatenate([first * cosine - second * sine, first * sine + second * cosine], axis=1)


def unrotate(values, cosine, sine):
    half = values.shape[1] // 2
    first, second = values[:, :half], values[:, half:]
    return jnp.concatenate([first * cosine + second * sine, second * cosine - first * sine], axis=1)


def on_device(
    plan,
    inputs,
    decay_exponent,
    first_gain,
    first_bias,
    query_weight,
    key_weight,
    value_weight,
    gate_weight,
    out_weight,
    second_gain,
    second_bias,
    up_weight,
    down_weight,
    cotangent,
):
    length, model = inputs.shape
    rows = query_weight.shape[0]
    pair_bit = lax.axis_index(plan.pair)
    column = lax.axis_index(plan.head_axes)
    width = cotangent.shape[1]

    key_size = query_weight.shape[1] // 2
    value_size = value_weight.shape[1] // 2
    hidden = up_weight.shape[1] // 2

    vectors = (first_gain, first_bias, second_gain, second_bias)

    exponent = jnp.where(pair_bit == 0, decay_exponent[0], decay_exponent[1]).astype(F32)
    lograte = jnp.log1p(-jnp.exp2(-exponent))
    offset = jnp.arange(length, dtype=F32)
    seq_index = lax.axis_index(plan.seq_axes)
    pair_weight = 2 ** plan.seq.index(plan.pair)
    first_slot = seq_index - pair_bit * pair_weight
    starts = jnp.stack([first_slot, first_slot + pair_weight]) * length
    frequency = np.exp(-math.log(10000.0) * np.arange(key_size // 2, dtype=np.float32) / (key_size // 2 - 1))
    frequency = frequency.astype(np.float32)
    angles = np.arange(length)[:, None] * frequency.astype(np.float64)[None, :]
    cos_off, sin_off = jnp.asarray(np.cos(angles), F32), jnp.asarray(np.sin(angles), F32)
    start_angles = starts.astype(F32)[:, None] * frequency[None, :]
    turn = jnp.stack([jnp.cos(start_angles), jnp.sin(start_angles)] * 4, axis=1)
    shards = [query_weight, key_weight, value_weight, gate_weight, out_weight, up_weight, down_weight]
    rate = jnp.full((8, 128), lograte, F32)
    f = front(plan, shards, inputs, cotangent, vectors, rate, turn, cos_off, sin_off, 1)
    b = back_pass(plan, f, cotangent, rate, turn, cos_off, sin_off, rows, 2)
    place = seq_index % (width // rows) * rows
    mine = lax.dynamic_slice_in_dim(b.sums_out, place, rows, 1)
    return (
        b.layer_out,
        b.grad_inputs,
        mine[0],
        mine[1],
        b.gq,
        b.gk,
        b.gv,
        b.gg,
        b.go,
        mine[2],
        mine[3],
        b.gu,
        b.gd,
    )


def solution(mesh):
    seq_bits = (mesh.shape["seq"]).bit_length() - 1
    head_bits = (mesh.shape["head"]).bit_length() - 1
    plan = Plan(seq_bits, head_bits)
    seq, head = plan.seq_axes, plan.head_axes
    fine = Mesh(mesh.devices.reshape((2,) * (seq_bits + head_bits)), seq + head)
    in_specs = (
        P(seq, None),
        P(head),
        P(seq),
        P(seq),
        P(seq, head),
        P(seq, head),
        P(seq, head),
        P(seq, head),
        P(head, seq),
        P(seq),
        P(seq),
        P(seq, head),
        P(head, seq),
        P(seq, head),
    )
    out_specs = (
        P(seq, head),
        P(seq, head),
        P(seq),
        P(seq),
        P(seq, head),
        P(seq, head),
        P(seq, head),
        P(seq, head),
        P(head, seq),
        P(seq),
        P(seq),
        P(seq, head),
        P(head, seq),
    )

    def step(*args):
        return on_device(plan, *args)

    return jax.shard_map(step, mesh=fine, in_specs=in_specs, out_specs=out_specs, check_vma=False)
```

profile of v0, /device:TPU:0, one launch (start us, length us, event | category | flops | bytes accessed | tf_op | source)
XLA Modules:
  0.0 445.1 jit_solution(9200032096432436274)
XLA Ops:
  0.7 0.1 fusion
  0.7 0.8 multiply_sine_fusion
  1.5 0.6 stack.11.refs_10_.refs_26_
  2.1 1.3 fusion.2
  4.8 0.6 broadcast_in_dim.16.refs_9_.refs_25_
  5.4 1.2 broadcast_in_dim.17.refs_13_
  6.6 1.2 broadcast_in_dim.18.refs_14_
  7.9 1.2 broadcast_in_dim.19.refs_15_
  9.1 1.2 broadcast_in_dim.20.refs_16_
  10.3 210.6 %front.1 = (bf16[2048,256]{1,0:T(8,128)(2,1)}, bf16[2048,256]{1,0:T(8,128)(2,1)}, bf16[2048,512]{1,0:T(8,128)(2,1)}, bf16[2048,512]{1,0:T(8,128)(2,1)}, bf16[204...) custom-call(bf16[256,512]{1,0:T(8,128)(2,1)} %refs_0_.1, ...), custom_call_target="tpu_custom_call" | custom-call | tf_op jit(solution)/shard_map/front/pallas_call | solution.py:875
  220.9 217.0 %back.1 = (bf16[6,2,256,512]{3,2,1,0:T(8,128)(2,1)}, bf16[2,512,2048]{2,1,0:T(8,128)(2,1)}, f32[512,512]{1,0:T(8,128)}, f32[512,512]{1,0:T(8,128)}, f32[8,512]{1,0:T(8,128)}) custom-call(bf16[2048,256]{1,0:T(8,128)(2,1)} %get-tuple-element.50.refs_0_, bf16[2048,256]{1,0:T(8,128)(2,1)} %get-tuple-element.51.refs_1_, ...), custom_call_target="tpu_custom_call" | custom-call | tf_op jit(solution)/shard_map/back/pallas_call | solution.py:1484
  438.0 5.6 %finish.1 = (f32[256,512]{1,0:T(8,128)}, f32[256,512]{1,0:T(8,128)}, f32[256,1024]{1,0:T(8,128)}, f32[256,1024]{1,0:T(8,128)}, f32[256,1024]{1,0:T(8,128)}, /*in...) custom-call(bf16[6,2,256,512]{3,2,1,0:T(8,128)(2,1)} %get-tuple-element.74.halves, ...), custom_call_target="tpu_custom_call" | custom-call | tf_op jit(solution)/shard_map/finish/pallas_call | solution.py:1539
  443.6 1.5 fusion.1
where the time goes:
time: 446 us; the launch traced here: 445 us
  Pallas kernels  433 us (97%)
  local copies, waits for them, and re-layouts  8.91 us (2%)
    pallas_call x1, Pallas kernels, back_pass(): pl.pallas_call(kernel, out_shape=tuple(far_outs.values()) + tuple(near_ou...  217 us
    pallas_call x1, Pallas kernels, front(): pl.pallas_call(functools.partial(front_kernel, plan, names), out_shape=tu...  211 us

commit v1 on v0

--- a/solution.py
+++ b/solution.py
@@ -561,9 +561,6 @@
     QUERY, KEY, VALUE, GATE, OUT, UP, DOWN = range(7)
     pair, high, low = [bulk.axes[0]], bulk.high, bulk.low
 
-    for row, vector in enumerate((r.gain_one, r.bias_one, r.gain_two, r.bias_two)):
-        r.vec[row : row + 1, :] = vector[...].astype(F32)
-    r.vec[4:8, :] = jnp.zeros((4, r.vec.shape[1]), F32)
     size = 1 << len(plan.seq)
     copies = []
     for mask in range(1, size):
@@ -767,7 +764,7 @@
         copy.wait()
 
 
-def front(plan, shards, inputs, cot, vectors, rate, turn, cos_off, sin_off, number):
+def front(plan, shards, inputs, cot, vec, rate, turn, cos_off, sin_off, number):
     length, model = inputs.shape
     width = cot.shape[1]
     size = 1 << len(plan.seq)
@@ -784,9 +781,7 @@
     if not flip:
         so, sd = so.T, sd.T
     far = dict(sq=sq, sk=sk, sv=sv, sg=sg, su=su)
-    near = dict(so=so, sd=sd, inputs=inputs, cot=cot, rate=rate, turn=turn, cos_off=cos_off, sin_off=sin_off)
-    gain_one, bias_one, gain_two, bias_two = [v[None] for v in vectors]
-    near.update(gain_one=gain_one, bias_one=bias_one, gain_two=gain_two, bias_two=bias_two)
+    near = dict(so=so, sd=sd, inputs=inputs, cot=cot, vec=vec, rate=rate, turn=turn, cos_off=cos_off, sin_off=sin_off)
     wq, wk, wv, wg, wu = [(model, s.shape[1] // 2) for s in far.values()]
     wo, wd = (model, value_size), (model, hidden)
     far_outs = dict(
@@ -847,7 +842,6 @@
         low_buf=carries[2],
         high_buf=carries[3],
         reach_bf=pltpu.VMEM((2, key_size, value_size), BF),
-        vec=pltpu.VMEM((8, rows), F32),
         vecs=pltpu.VMEM((size, 8, rows), F32),
         stats=pltpu.VMEM((4, 8, length), F32),
         hand=hand,
@@ -1591,9 +1585,9 @@
     value_size = value_weight.shape[1] // 2
     hidden = up_weight.shape[1] // 2
 
-    vectors = (first_gain, first_bias, second_gain, second_bias)
-
-    exponent = jnp.where(pair_bit == 0, decay_exponent[0], decay_exponent[1]).astype(F32)
+    vec = jnp.stack([first_gain, first_bias, second_gain, second_bias] * 2).astype(F32)
+
+    exponent = pick(decay_exponent, pair_bit, 0).astype(F32)
     lograte = jnp.log1p(-jnp.exp2(-exponent))
     offset = jnp.arange(length, dtype=F32)
     seq_index = lax.axis_index(plan.seq_axes)
@@ -1608,7 +1602,7 @@
     turn = jnp.stack([jnp.cos(start_angles), jnp.sin(start_angles)] * 4, axis=1)
     shards = [query_weight, key_weight, value_weight, gate_weight, out_weight, up_weight, down_weight]
     rate = jnp.full((8, 128), lograte, F32)
-    f = front(plan, shards, inputs, cotangent, vectors, rate, turn, cos_off, sin_off, 1)
+    f = front(plan, shards, inputs, cotangent, vec, rate, turn, cos_off, sin_off, 1)
     b = back_pass(plan, f, cotangent, rate, turn, cos_off, sin_off, rows, 2)
     place = seq_index % (width // rows) * rows
     mine = lax.dynamic_slice_in_dim(b.sums_out, place, rows, 1)

time: 446 us -> 444 us (level)
    broadcast_in_dim x4 -> x0, local copies, waits for them, and re-layouts: 4.88 us -> none  [front(): gain_one, bias_one, gain_two, bias_two = [v[None] for v in vectors]]
where the time goes in v1:
time: 444 us; the launch traced here: 443 us
  Pallas kernels  433 us (98%)
  local copies, waits for them, and re-layouts  6.62 us (1%)
    pallas_call x1, Pallas kernels, back_pass(): pl.pallas_call(kernel, out_shape=tuple(far_outs.values()) + tuple(near_ou...  217 us
    pallas_call x1, Pallas kernels, front(): pl.pallas_call(functools.partial(front_kernel, plan, names), out_shape=tu...  211 us

profile of v1, /device:TPU:0, one launch (start us, length us, event | category | flops | bytes accessed | tf_op | source)
XLA Modules:
  0.0 442.8 jit_solution(5260211429701574144)
XLA Ops:
  0.7 0.1 fusion
  0.7 0.8 multiply_sine_fusion
  1.5 0.6 stack.47.refs_11_.refs_26_
  2.1 1.2 dynamic_slice.7
  4.1 0.6 broadcast_in_dim.4.refs_10_.refs_25_
  4.7 0.7 stack.18
  5.4 0.7 stack.19
  6.0 0.7 stack.20
  6.7 0.7 stack.42
  7.4 0.6 convert_element_type.14.refs_9_
  8.0 210.6 %front.1 = (bf16[2048,256]{1,0:T(8,128)(2,1)}, bf16[2048,256]{1,0:T(8,128)(2,1)}, bf16[2048,512]{1,0:T(8,128)(2,1)}, bf16[2048,512]{1,0:T(8,128)(2,1)}, bf16[204...) custom-call(bf16[256,512]{1,0:T(8,128)(2,1)} %refs_0_.1, ...), custom_call_target="tpu_custom_call" | custom-call | tf_op jit(solution)/shard_map/front/pallas_call | solution.py:869
  218.6 217.1 %back.1 = (bf16[6,2,256,512]{3,2,1,0:T(8,128)(2,1)}, bf16[2,512,2048]{2,1,0:T(8,128)(2,1)}, f32[512,512]{1,0:T(8,128)}, f32[512,512]{1,0:T(8,128)}, f32[8,512]{1,0:T(8,128)}) custom-call(bf16[2048,256]{1,0:T(8,128)(2,1)} %get-tuple-element.50.refs_0_, bf16[2048,256]{1,0:T(8,128)(2,1)} %get-tuple-element.51.refs_1_, ...), custom_call_target="tpu_custom_call" | custom-call | tf_op jit(solution)/shard_map/back/pallas_call | solution.py:1478
  435.7 5.6 %finish.1 = (f32[256,512]{1,0:T(8,128)}, f32[256,512]{1,0:T(8,128)}, f32[256,1024]{1,0:T(8,128)}, f32[256,1024]{1,0:T(8,128)}, f32[256,1024]{1,0:T(8,128)}, /*in...) custom-call(bf16[6,2,256,512]{3,2,1,0:T(8,128)(2,1)} %get-tuple-element.74.halves, ...), custom_call_target="tpu_custom_call" | custom-call | tf_op jit(solution)/shard_map/finish/pallas_call | solution.py:1533
  441.3 1.5 fusion.1
  (1 shorter events, 0.0 us)
